TPU v7x, 32 devices: a whole 2x2x4 slice. The times are simulated.
32 devices in a mesh: band: 8 (over z, y), sub: 4 (over x, core).
Axes of the slice: x: 2, y: 2, z: 4, core: 2. Of those that a mesh axis runs over, the one named last changes fastest.
Arguments:
- grid_x: bfloat16 [227, 16384], P(None, ('band', 'sub')), may hold values from -6 to 6
- mesh_in: bfloat16 [2048, 512], P(('band', 'sub')), may hold values from -6 to 6
- w_embed: bfloat16 [227, 512], replicated, may hold values from -0.375 to 0.375
- w_src: bfloat16 [512, 512], replicated, may hold values from -0.25 to 0.25
- w_dst: bfloat16 [512, 512], replicated, may hold values from -0.25 to 0.25
- w_edge: bfloat16 [512, 512], replicated, may hold values from -0.25 to 0.25
- w_proc: bfloat16 [512, 512], replicated, may hold values from -0.25 to 0.25
- w_recv: bfloat16 [512, 512], replicated, may hold values from -0.25 to 0.25
- g2m_src: int32 [2048, 40], P(('band', 'sub')), may hold values from 0 to 16383, as said below
- mesh_src: int32 [2048, 6], P(('band', 'sub')), may hold values from 0 to 2047, as said below
- cotangent: bfloat16 [2048, 512], P(('band', 'sub')), may hold values from -6 to 6
Outputs:
- mesh_out: bfloat16 [2048, 512], P(('band', 'sub'))
- grid_grad: float32 [227, 16384], P(None, ('band', 'sub'))
- src_grad: float32 [512, 512], replicated
- edge_grad: float32 [512, 512], replicated
Inputs may be any that keep to these rules, and one draw needn't show every extreme that they name: Grid node g belongs to band g // (512 * 4), mesh node m to band m // (64 * 4); g2m_src[m, k] lies in the band of mesh node m, or among the 512 grid nodes of an adjacent band that stand next to that band in index order. mesh_src[m, j] lies in the band of mesh node m, or among the 64 mesh nodes of an adjacent band that stand next to that band in index order.
All inputs are finite; a program needn't handle non-finite values.
Results may differ from a plain program's by a relative error of at most 0.015.
Values may be sent and summed in bfloat16 or wider, within the bound.
A program may use at most 128 MiB of HBM per device.

v0:
```python
import math
import jax
import jax.numpy as jnp
from jax import lax
from jax.sharding import PartitionSpec as P

EPSILON = 1e-05


def padded(shard, sides, width):
    for axis, dim in sides:
        devices, length = (lax.axis_size(axis), shard.shape[dim])
        up = [(i, (i + 1) % devices) for i in range(devices - 1)]
        down = [(j, i) for i, j in up]
        last = lax.slice_in_dim(shard, length - width, length, axis=dim)
        first = lax.slice_in_dim(shard, 0, width, axis=dim)
        before = lax.ppermute(last, axis, up)
        after = lax.ppermute(first, axis, down)
        shard = jnp.concatenate([before, shard, after], axis=dim)
    return shard


def from_behind(value, axis, steps):
    count = lax.axis_size(axis)
    first, last = (max(0, -steps), min(count, count - steps))
    return lax.ppermute(value, axis, [(source, source + steps) for source in range(first, last)])


def silu_slope(value):
    sigma = jax.nn.sigmoid(value)
    return sigma * (1.0 + value * (1.0 - sigma))


def normalize(value):
    centred = value - jnp.mean(value, axis=-1, keepdims=True)
    spread = jnp.sqrt(jnp.mean(centred * centred, axis=-1, keepdims=True) + EPSILON)
    return (centred / spread, spread)


def times_transpose(left, right):
    return lax.dot_general(
        left, right, (((1,), (1,)), ((), ())), preferred_element_type=jnp.float32
    )


def first_contract(left, right):
    return lax.dot_general(
        left, right, (((0,), (0,)), ((), ())), preferred_element_type=jnp.float32
    )


def fetch_grid(projected):
    border = projected.shape[0]
    block = lax.all_gather(projected, "sub", axis=0, tiled=True)
    return padded(block, (("band", 0),), border)


def return_grid(window_grad, border):
    middle = window_grad[border:-border]
    from_above = from_behind(window_grad[:border].astype(jnp.bfloat16), "band", -1).astype(
        jnp.float32
    )
    from_below = from_behind(window_grad[-border:].astype(jnp.bfloat16), "band", 1).astype(
        jnp.float32
    )
    middle = middle.at[:border].add(from_below)
    middle = middle.at[middle.shape[0] - border :].add(from_above)
    return lax.psum_scatter(
        middle.astype(jnp.bfloat16), "sub", scatter_dimension=0, tiled=True
    ).astype(jnp.float32)


def return_mesh(window_grad, border):
    middle = window_grad[border:-border]
    from_above = from_behind(window_grad[:border].astype(jnp.bfloat16), "band", -1).astype(
        jnp.float32
    )
    from_below = from_behind(window_grad[-border:].astype(jnp.bfloat16), "band", 1).astype(
        jnp.float32
    )
    middle = middle.at[:border].add(from_below)
    middle = middle.at[middle.shape[0] - border :].add(from_above)
    return lax.psum_scatter(
        middle.astype(jnp.bfloat16), "sub", scatter_dimension=0, tiled=True
    ).astype(jnp.float32)


def body(
    grid_x, mesh_in, w_embed, w_src, w_dst, w_edge, w_proc, w_recv, g2m_src, mesh_src, cotangent
):
    latent = w_src.shape[0]
    mesh_rows, enc_count = g2m_src.shape
    mesh_count = mesh_src.shape[1]
    band_index = lax.axis_index("band")
    groups = lax.axis_size("sub")
    hidden_pre = first_contract(grid_x, w_embed)
    hidden_grid = jax.nn.silu(hidden_pre).astype(jnp.bfloat16)
    projected = jnp.dot(hidden_grid, w_src, preferred_element_type=jnp.float32).astype(jnp.bfloat16)
    dest_term = jnp.dot(mesh_in, w_dst, preferred_element_type=jnp.float32)
    grid_border = projected.shape[0]
    grid_window = fetch_grid(projected)
    grid_base = band_index * (grid_border * groups) - grid_border
    grid_local = (g2m_src - grid_base).reshape(-1)
    before = jnp.take(grid_window, grid_local, axis=0).astype(jnp.float32)
    before = (before.reshape(mesh_rows, enc_count, latent) + dest_term[:, None, :]).reshape(
        -1, latent
    )
    active = jax.nn.silu(before).astype(jnp.bfloat16)
    normed, spread = normalize(jnp.dot(active, w_edge, preferred_element_type=jnp.float32))
    encoded = jnp.sum(normed.reshape(mesh_rows, enc_count, latent), axis=1)
    hidden_mesh = (mesh_in.astype(jnp.float32) + encoded / math.sqrt(enc_count)).astype(
        jnp.bfloat16
    )
    query = jnp.dot(hidden_mesh, w_proc, preferred_element_type=jnp.float32).astype(jnp.bfloat16)
    receiver = jnp.dot(hidden_mesh, w_recv, preferred_element_type=jnp.float32)
    mesh_border = query.shape[0]
    mesh_block = lax.all_gather(query, "sub", axis=0, tiled=True)
    mesh_window = padded(mesh_block, (("band", 0),), mesh_border)
    mesh_base = band_index * mesh_block.shape[0] - mesh_border
    mesh_local = (mesh_src - mesh_base).reshape(-1)
    mesh_before = jnp.take(mesh_window, mesh_local, axis=0).astype(jnp.float32)
    mesh_before = mesh_before.reshape(mesh_rows, mesh_count, latent) + receiver[:, None, :]
    summed = jnp.sum(jax.nn.silu(mesh_before), axis=1)
    mesh_out = (hidden_mesh.astype(jnp.float32) + summed / math.sqrt(mesh_count)).astype(
        jnp.bfloat16
    )
    upstream = cotangent.astype(jnp.float32)
    mesh_slope = (upstream / math.sqrt(mesh_count))[:, None, :] * silu_slope(mesh_before)
    receiver_grad = jnp.sum(mesh_slope, axis=1)
    window_grad = jnp.zeros((mesh_window.shape[0], latent), jnp.float32)
    window_grad = window_grad.at[mesh_local].add(mesh_slope.reshape(-1, latent))
    query_grad = return_mesh(window_grad, mesh_border)
    mesh_grad = upstream + times_transpose(query_grad.astype(jnp.bfloat16), w_proc)
    mesh_grad = mesh_grad + times_transpose(receiver_grad.astype(jnp.bfloat16), w_recv)
    upper = mesh_grad / math.sqrt(enc_count)
    incoming = jnp.broadcast_to(upper[:, None, :], (mesh_rows, enc_count, latent)).reshape(
        -1, latent
    )
    centred_grad = incoming - jnp.mean(incoming, axis=-1, keepdims=True)
    centred_grad = centred_grad - normed * jnp.mean(incoming * normed, axis=-1, keepdims=True)
    norm_grad = (centred_grad / spread).astype(jnp.bfloat16)
    edge_part = first_contract(active, norm_grad)
    before_grad = times_transpose(norm_grad, w_edge) * silu_slope(before)
    grid_window_grad = (
        jnp.zeros((grid_window.shape[0], latent), jnp.float32).at[grid_local].add(before_grad)
    )
    projected_grad = return_grid(grid_window_grad, grid_border)
    projected_low = projected_grad.astype(jnp.bfloat16)
    src_part = first_contract(hidden_grid, projected_low)
    hidden_grad = (times_transpose(projected_low, w_src) * silu_slope(hidden_pre)).astype(
        jnp.bfloat16
    )
    grid_grad = times_transpose(w_embed, hidden_grad)
    src_grad, edge_grad = lax.psum((src_part, edge_part), ("band", "sub"))
    return (mesh_out, grid_grad, src_grad, edge_grad)


def solution(mesh):
    placed = (
        P(None, ("band", "sub")),
        P(("band", "sub"), None),
        P(),
        P(),
        P(),
        P(),
        P(),
        P(),
        P(("band", "sub"), None),
        P(("band", "sub"), None),
        P(("band", "sub"), None),
    )
    return jax.shard_map(
        body,
        mesh=mesh,
        in_specs=placed,
        out_specs=(P(("band", "sub"), None), P(None, ("band", "sub")), P(), P()),
        check_vma=False,
    )
```

profile of v0, /device:TPU:0, one launch (start us, length us, event | category | flops | bytes accessed | tf_op | source)
XLA Modules:
  0.0 408.9 jit_solution(17956858091147088192)
XLA Ops:
  7.3 1.4 fusion.53
  8.7 1.0 copy-done.8
  9.7 2.4 convolution_convert_fusion
  12.4 0.6 compare_and_fusion.1
  13.4 0.6 copy-done.6
  14.2 1.0 mul.82
  15.3 0.6 compare_and_fusion.2
  15.9 21.6 %all-gather.2.cloned.1.call-done = bf16[2048,512]{1,0:T(8,128)(2,1)} async-done(((bf16[512,512]{1,0:T(8,128)(2,1)}), bf16[2048,512]{1,0:T(8,128)(2,1)}) %all-gather.2.cloned.1.call-update) | async-done | bytes 2097168 | tf_op jit(solution)/shard_map/all_gather | solution.py:54
  37.5 1.3 fusion.48
  38.8 3.4 collective-permute-start
  42.2 1.3 collective-permute-start.1
  43.6 0.2 fusion.54
  43.8 21.2 %collective-permute-done = bf16[512,512]{1,0:T(8,128)(2,1)S(1)} collective-permute-done((bf16[512,512]{1,0:T(8,128)(2,1)S(1)}, bf16[512,512]{1,0:T(8,128)(2,1)S(1)}, u32[]{:S(2)}, u32[]{:S(2)}) %collective-permute-start) | collective-permute-done | bytes 524320 | tf_op jit(solution)/shard_map/ppermute | solution.py:17
  65.0 3.0 pad_maximum_fusion
  67.9 10.6 %gather_fusion = bf16[2560,512]{1,0:T(8,128)(2,1)} fusion(bf16[3072,512]{1,0:T(8,128)(2,1)} %pad_maximum_fusion, s32[3072]{0:T(1024)S(1)} %pad_clamp_fusion), kind=kCustom, calls=%fused_computation | custom fusion | bytes 5253120 | tf_op jit(solution)/shard_map/jit(_take)/gather | solution.py:104
  78.6 5.7 %bitcast_add_fusion = (f32[2560,512]{1,0:T(8,128)}, bf16[2560,512]{1,0:T(8,128)(2,1)S(1)}) fusion(f32[64,512]{1,0:T(8,128)S(1)} %fusion.54, bf16[2560,512]{1,0:T(8,128)(2,1)} %gather_fusion, pred[2560]{0:T(1024)(128)(4,1)S(1)} %compare_and_fusion), kind=kLoop, calls=%fused_computation.10 | loop fusion | flops 10485760 | bytes 10619392 | tf_op jit(solution)/shard_map/add | solution.py:105
  84.2 1.6 fusion.51
  85.8 0.9 multiply_reduce_fusion
  86.8 3.4 subtract_divide_fusion
  90.3 3.4 reduce_sum.67
  93.7 1.3 convolution_convert_fusion.1
  95.0 5.8 %all_gather.7 = bf16[256,512]{1,0:T(8,128)(2,1)S(1)} all-gather(bf16[64,512]{1,0:T(8,128)(2,1)S(1)} %convolution_convert_fusion.1), channel_id=1, replica_groups=mesh['band'=8,'sub'=4] {'sub'}, dimensions={0}, use_global_device_ids=true | all-gather | bytes 327680 | tf_op jit(solution)/shard_map/all_gather | solution.py:117
  100.8 0.7 copy-done.5
  101.5 4.4 %collective-permute-start.2 = (bf16[64,512]{1,0:T(8,128)(2,1)S(1)}, bf16[64,512]{1,0:T(8,128)(2,1)S(1)}, u32[]{:S(2)}, u32[]{:S(2)}) collective-permute-start(bf16[64,512]{1,0:T(8,128)(2,1)S(1)} %get-tuple-element.66), channel_id=1, source_target_pairs={{0,4},{4,8},{8,12},{12,16},{16,20},{20,24},{24,28},{1,5},{5,9},{9,... | collective-permute-start | bytes 196616 | tf_op jit(solution)/shard_map/ppermute | solution.py:17
  105.9 1.5 collective-permute-start.3
  107.4 1.2 fusion.55
  108.6 0.6 copy-done.7
  109.3 1.1 add.186
  110.4 2.2 add.192
  112.6 0.6 copy-done.20
  113.2 1.0 pad_maximum_fusion.1
  114.3 2.6 gather_fusion.1
  116.9 5.1 %scatter_custom_fusion = f32[384,512]{1,0:T(8,128)} fusion(s32[384]{0:T(512)} %copy-done.23, f32[384,512]{1,0:T(8,128)} %mul.82, f32[384,512]{1,0:T(8,128)} %add.192, bf16[384,512]{1,0:T(8,128)(2,1)} %gather_fusion.1, f32[]{:T(128)} %constant.173.clone.1, f32[]{:T(128)} %constant.175.clone.1, pred[384]{0:T(512)(128)(4,1)} %compare_and_fusion.2, ...), kind=kCustom, calls=%fused_computation.47 | custom fusion | flops 2359296 | bytes 2754560 | tf_op jit(solution)/shard_map/scatter-add | solution.py:131
  121.9 1.2 convert.8
  123.1 4.9 %collective-permute-start.4 = (bf16[64,512]{1,0:T(8,128)(2,1)S(1)}, bf16[64,512]{1,0:T(8,128)(2,1)S(1)}, u32[]{:S(2)}, u32[]{:S(2)}) collective-permute-start(bf16[64,512]{1,0:T(8,128)(2,1)S(1)} %get-tuple-element.65), channel_id=1, source_target_pairs={{0,4},{4,8},{8,12},{12,16},{16,20},{20,24},{24,28},{1,5},{5,9},{9,... | collective-permute-start | bytes 196616 | tf_op jit(solution)/shard_map/ppermute | solution.py:26
  128.0 1.1 slice.134
  129.1 1.3 collective-permute-start.5
  130.4 0.9 fusion.41
  131.4 4.8 %collective-permute-done.5 = bf16[64,512]{1,0:T(8,128)(2,1)S(1)} collective-permute-done((bf16[64,512]{1,0:T(8,128)(2,1)S(1)}, bf16[64,512]{1,0:T(8,128)(2,1)S(1)}, u32[]{:S(2)}, u32[]{:S(2)}) %collective-permute-start.5) | collective-permute-done | bytes 65568 | tf_op jit(solution)/shard_map/ppermute | solution.py:26
  136.2 0.8 convert_element_type.88
  137.1 0.7 copy.18
  137.8 0.9 gather.12
  138.7 2.9 multiply_reduce_fusion.1
  141.6 16.1 %reduce-scatter.3.cloned.1.call-done = bf16[64,512]{1,0:T(8,128)(2,1)} async-done(((bf16[256,512]{1,0:T(8,128)(2,1)}), bf16[64,512]{1,0:T(8,128)(2,1)}) %reduce-scatter.3.cloned.1.call-update) | async-done | bytes 65552 | tf_op jit(solution)/shard_map/reduce_scatter | solution.py:83
  157.7 1.3 convolution_add_fusion.1
  159.0 1.4 fusion.52
  160.5 3.6 fusion.3
  164.3 3.9 fusion.2
  168.2 3.9 fusion.56
  172.2 21.5 %scatter_custom_fusion.1 = f32[3072,512]{1,0:T(8,128)} fusion(s32[2560]{0:T(1024)} %copy-done.21, f32[2560,512]{1,0:T(8,128)} %fusion.56, f32[2560,512]{1,0:T(8,128)} %get-tuple-element.60, f32[]{:T(128)} %constant.175.clone.1, f32[]{:T(128)} %constant.173.clone.1), kind=kCustom, calls=%fused_computation.11 | custom fusion | flops 11796480 | bytes 16778240 | tf_op jit(solution)/shard_map/scatter-add | solution.py:145
  193.7 3.2 convert.9
  197.0 3.7 collective-permute-start.6
  200.7 1.3 collective-permute-start.7
  202.0 21.0 %collective-permute-done.6 = bf16[512,512]{1,0:T(8,128)(2,1)S(1)} collective-permute-done((bf16[512,512]{1,0:T(8,128)(2,1)S(1)}, bf16[512,512]{1,0:T(8,128)(2,1)S(1)}, u32[]{:S(2)}, u32[]{:S(2)}) %collective-permute-start.6) | collective-permute-done | bytes 524320 | tf_op jit(solution)/shard_map/ppermute | solution.py:26
  223.2 0.3 fusion.16
  223.5 1.6 convert_element_type.93
  225.1 4.2 %fusion.57 = f32[512,512]{1,0:T(8,128)} fusion(bf16[2560,512]{1,0:T(8,128)(2,1)S(1)} %get-tuple-element.61, bf16[2560,512]{1,0:T(8,128)(2,1)} %copy-done.3), kind=kOutput, calls=%fused_computation.105 | convolution fusion | flops 1342177280 | bytes 6291456 | tf_op jit(solution)/shard_map/dot_general | solution.py:47
  229.4 27.8 %reduce-scatter.5.cloned.1.call-done = bf16[512,512]{1,0:T(8,128)(2,1)} async-done(((bf16[2048,512]{1,0:T(8,128)(2,1)}), bf16[512,512]{1,0:T(8,128)(2,1)}) %reduce-scatter.5.cloned.1.call-update) | async-done | bytes 524304 | tf_op jit(solution)/shard_map/reduce_scatter | solution.py:68
  257.2 2.9 fusion.46
  260.1 0.6 add_convert_fusion
  260.8 1.7 fusion.14
  262.5 135.4 %all-reduce.3.cloned.1.call-done = (f32[512,512]{1,0:T(8,128)}, f32[512,512]{1,0:T(8,128)}) async-done(((f32[512,512]{1,0:T(8,128)}, f32[512,512]{1,0:T(8,128)}), (f32[512,512]{1,0:T(8,128)}, f32[512,512]{1,0:T(8,128)})) %all-reduce.3.cloned.1.call-update) | async-done | bytes 2097168 | tf_op jit(solution)/shard_map/psum | solution.py:154
  397.8 2.3 copy.27
  400.1 2.3 copy.28
  (92 shorter events, 1.7 us)
Async XLA Ops:
  7.2 77.1 %copy-start = (bf16[512,512]{1,0:T(8,128)(2,1)S(1)}, bf16[512,512]{1,0:T(8,128)(2,1)}, u32[]{:S(2)}) copy-start(bf16[512,512]{1,0:T(8,128)(2,1)} %param.24) | copy-start | bytes 1572868
  7.2 4.9 %copy-start.22 = (s32[64,40]{0,1:T(8,128)S(1)}, s32[64,40]{0,1:T(8,128)}, u32[]{:S(2)}) copy-start(s32[64,40]{0,1:T(8,128)} %param.27) | copy-start | bytes 30724
  7.2 5.2 %copy-start.25 = (s32[64,6]{0,1:T(8,128)S(1)}, s32[64,6]{0,1:T(8,128)}, u32[]{:S(2)}) copy-start(s32[64,6]{0,1:T(8,128)} %param.28) | copy-start | bytes 4612
  7.2 6.2 %copy-start.14 = (bf16[64,512]{1,0:T(8,128)(2,1)S(1)}, bf16[64,512]{1,0:T(8,128)(2,1)}, u32[]{:S(2)}) copy-start(bf16[64,512]{1,0:T(8,128)(2,1)} %param.29) | copy-start | bytes 196612
  7.2 30.3 %all-gather.2.cloned.1.call-start = ((), (), s32[]{:S(2)}) async-start(), calls=%async_computation.2 | async-start | bytes 2621440 | tf_op jit(solution)/shard_map/all_gather | solution.py:54
  8.7 1.0 copy-start.8
  9.7 33.9 %copy-start.13 = (bf16[512,512]{1,0:T(8,128)(2,1)S(1)}, bf16[512,512]{1,0:T(8,128)(2,1)}, u32[]{:S(2)}) copy-start(bf16[512,512]{1,0:T(8,128)(2,1)} %param.23) | copy-start | bytes 1572868
  9.7 33.9 %copy-start.15 = (bf16[64,512]{1,0:T(8,128)(2,1)S(1)}, bf16[64,512]{1,0:T(8,128)(2,1)}, u32[]{:S(2)}) copy-start(bf16[64,512]{1,0:T(8,128)(2,1)} %param.20) | copy-start | bytes 196612
  12.1 145.7 %reduce-scatter.3.cloned.1.call-start = ((), (), s32[]{:S(2)}) async-start(), calls=%async_computation.3 | async-start | bytes 327680 | tf_op jit(solution)/shard_map/reduce_scatter | solution.py:83
  13.4 0.7 copy-start.6
  15.2 52.7 %copy-start.21 = (s32[2560]{0:T(1024)}, s32[2560]{0:T(1024)S(1)}, u32[]{:S(2)}) copy-start(s32[2560]{0:T(1024)S(1)} %fusion.43) | copy-start | bytes 30724
  15.3 28.2 %copy-start.23 = (s32[384]{0:T(512)}, s32[384]{0:T(512)S(1)}, u32[]{:S(2)}) copy-start(s32[384]{0:T(512)S(1)} %fusion.44) | copy-start | bytes 4612
  38.8 26.2 %collective-permute-start = (bf16[512,512]{1,0:T(8,128)(2,1)S(1)}, bf16[512,512]{1,0:T(8,128)(2,1)S(1)}, u32[]{:S(2)}, u32[]{:S(2)}) collective-permute-start(bf16[512,512]{1,0:T(8,128)(2,1)S(1)} %get-tuple-element.62), channel_id=1, source_target_pairs={{0,4},{4,8},{8,12},{12,16},{16,20},{20,24},{24,28},{1,5},{5,9},{9,... | collective-permute-start | bytes 1572872 | tf_op jit(solution)/shard_map/ppermute | solution.py:17
  42.2 22.8 %collective-permute-start.1 = (bf16[512,512]{1,0:T(8,128)(2,1)S(1)}, bf16[512,512]{1,0:T(8,128)(2,1)S(1)}, u32[]{:S(2)}, u32[]{:S(2)}) collective-permute-start(bf16[512,512]{1,0:T(8,128)(2,1)S(1)} %get-tuple-element.63), channel_id=1, source_target_pairs={{4,0},{8,4},{12,8},{16,12},{20,16},{24,20},{28,24},{5,1},{9,5},{13... | collective-permute-start | bytes 1572872 | tf_op jit(solution)/shard_map/ppermute | solution.py:18
  85.8 4.4 %copy-start.1 = (f32[2560,512]{1,0:T(8,128)}, f32[2560,512]{1,0:T(8,128)S(1)}, u32[]{:S(2)}) copy-start(f32[2560,512]{1,0:T(8,128)S(1)} %get-tuple-element.69) | copy-start | bytes 15728644
  86.8 3.5 copy-start.18
  90.3 3.4 copy-start.16
  93.7 13.7 %copy-start.10 = (bf16[64,512]{1,0:T(8,128)(2,1)}, bf16[64,512]{1,0:T(8,128)(2,1)S(1)}, u32[]{:S(2)}) copy-start(bf16[64,512]{1,0:T(8,128)(2,1)S(1)} %add_convert_fusion.1) | copy-start | bytes 196612
  100.8 0.7 copy-start.5
  101.5 11.1 %collective-permute-start.2 = (bf16[64,512]{1,0:T(8,128)(2,1)S(1)}, bf16[64,512]{1,0:T(8,128)(2,1)S(1)}, u32[]{:S(2)}, u32[]{:S(2)}) collective-permute-start(bf16[64,512]{1,0:T(8,128)(2,1)S(1)} %get-tuple-element.66), channel_id=1, source_target_pairs={{0,4},{4,8},{8,12},{12,16},{16,20},{20,24},{24,28},{1,5},{5,9},{9,... | collective-permute-start | bytes 196616 | tf_op jit(solution)/shard_map/ppermute | solution.py:17
  105.9 7.4 %collective-permute-start.3 = (bf16[64,512]{1,0:T(8,128)(2,1)S(1)}, bf16[64,512]{1,0:T(8,128)(2,1)}, u32[]{:S(2)}, u32[]{:S(2)}) collective-permute-start(bf16[64,512]{1,0:T(8,128)(2,1)S(1)} %get-tuple-element.67), channel_id=1, source_target_pairs={{4,0},{8,4},{12,8},{16,12},{20,16},{24,20},{28,24},{5,1},{9,5},{13... | collective-permute-start | bytes 196616 | tf_op jit(solution)/shard_map/ppermute | solution.py:18
  108.6 0.6 copy-start.7
  112.6 0.6 copy-start.20
  116.8 20.2 %copy-start.24 = (pred[64,6]{0,1:T(8,128)(4,1)S(1)}, pred[64,6]{0,1:T(8,128)(4,1)}, u32[]{:S(2)}) copy-start(pred[64,6]{0,1:T(8,128)(4,1)} %get-tuple-element.56) | copy-start | bytes 1156
  116.9 20.9 %copy-start.4 = (bf16[384,512]{1,0:T(8,128)(2,1)S(1)}, bf16[384,512]{1,0:T(8,128)(2,1)}, u32[]{:S(2)}) copy-start(bf16[384,512]{1,0:T(8,128)(2,1)} %gather_fusion.1) | copy-start | bytes 1179652
  123.1 7.3 %collective-permute-start.4 = (bf16[64,512]{1,0:T(8,128)(2,1)S(1)}, bf16[64,512]{1,0:T(8,128)(2,1)S(1)}, u32[]{:S(2)}, u32[]{:S(2)}) collective-permute-start(bf16[64,512]{1,0:T(8,128)(2,1)S(1)} %get-tuple-element.65), channel_id=1, source_target_pairs={{0,4},{4,8},{8,12},{12,16},{16,20},{20,24},{24,28},{1,5},{5,9},{9,... | collective-permute-start | bytes 196616 | tf_op jit(solution)/shard_map/ppermute | solution.py:26
  129.1 7.1 %collective-permute-start.5 = (bf16[64,512]{1,0:T(8,128)(2,1)S(1)}, bf16[64,512]{1,0:T(8,128)(2,1)S(1)}, u32[]{:S(2)}, u32[]{:S(2)}) collective-permute-start(bf16[64,512]{1,0:T(8,128)(2,1)S(1)} %get-tuple-element.64), channel_id=1, source_target_pairs={{4,0},{8,4},{12,8},{16,12},{20,16},{24,20},{28,24},{5,1},{9,5},{13... | collective-permute-start | bytes 196616 | tf_op jit(solution)/shard_map/ppermute | solution.py:26
  137.0 120.2 %reduce-scatter.5.cloned.1.call-start = ((), (), s32[]{:S(2)}) async-start(), calls=%async_computation.4 | async-start | bytes 2621440 | tf_op jit(solution)/shard_map/reduce_scatter | solution.py:68
  138.7 25.6 %copy-start.19 = (f32[2560]{0:T(1024)S(1)}, f32[2560]{0:T(1024)}, u32[]{:S(2)}) copy-start(f32[2560]{0:T(1024)} %copy-done.18) | copy-start | bytes 30724
  168.2 4.0 copy-start.3
  196.9 26.1 %copy-start.2 = (f32[3072,512]{1,0:T(8,128)S(1)}, f32[3072,512]{1,0:T(8,128)}, u32[]{:S(2)}) copy-start(f32[3072,512]{1,0:T(8,128)} %scatter_custom_fusion.1) | copy-start | bytes 18874372
  196.9 26.1 %slice-start = ((f32[3072,512]{1,0:T(8,128)}), f32[2048,512]{1,0:T(8,128)S(1)}, s32[]{:S(2)}) async-start(f32[3072,512]{1,0:T(8,128)} %scatter_custom_fusion.1), calls=%async_computation.6 | async-start | bytes 8388608 | tf_op jit(solution)/shard_map/slice | solution.py:59
  197.0 26.0 %collective-permute-start.6 = (bf16[512,512]{1,0:T(8,128)(2,1)S(1)}, bf16[512,512]{1,0:T(8,128)(2,1)S(1)}, u32[]{:S(2)}, u32[]{:S(2)}) collective-permute-start(bf16[512,512]{1,0:T(8,128)(2,1)S(1)} %get-tuple-element.59), channel_id=1, source_target_pairs={{0,4},{4,8},{8,12},{12,16},{16,20},{20,24},{24,28},{1,5},{5,9},{9,... | collective-permute-start | bytes 1572872 | tf_op jit(solution)/shard_map/ppermute | solution.py:26
  200.7 22.5 %collective-permute-start.7 = (bf16[512,512]{1,0:T(8,128)(2,1)S(1)}, bf16[512,512]{1,0:T(8,128)(2,1)S(1)}, u32[]{:S(2)}, u32[]{:S(2)}) collective-permute-start(bf16[512,512]{1,0:T(8,128)(2,1)S(1)} %get-tuple-element.58), channel_id=1, source_target_pairs={{4,0},{8,4},{12,8},{16,12},{20,16},{24,20},{28,24},{5,1},{9,5},{13... | collective-permute-start | bytes 1572872 | tf_op jit(solution)/shard_map/ppermute | solution.py:26
  225.1 172.7 %all-reduce.3.cloned.1.call-start = ((), (), s32[]{:S(2)}) async-start(), calls=%async_computation.5 | async-start | bytes 4194304 | tf_op jit(solution)/shard_map/psum | solution.py:154
  229.4 30.7 %copy-start.11 = (bf16[64,512]{1,0:T(8,128)(2,1)S(1)}, bf16[64,512]{1,0:T(8,128)(2,1)}, u32[]{:S(2)}) copy-start(bf16[64,512]{1,0:T(8,128)(2,1)} %copy-done.10) | copy-start | bytes 196612
  229.4 30.7 %copy-start.12 = (f32[64,512]{1,0:T(8,128)S(1)}, f32[64,512]{1,0:T(8,128)}, u32[]{:S(2)}) copy-start(f32[64,512]{1,0:T(8,128)} %get-tuple-element.53) | copy-start | bytes 393220
  229.4 31.4 %copy-start.9 = (f32[512,512]{1,0:T(8,128)S(1)}, f32[512,512]{1,0:T(8,128)}, u32[]{:S(2)}) copy-start(f32[512,512]{1,0:T(8,128)} %copy-done.8) | copy-start | bytes 3145732
  229.4 31.4 %copy-start.17 = (bf16[227,512]{1,0:T(8,128)(2,1)S(1)}, bf16[227,512]{1,0:T(8,128)(2,1)}, u32[]{:S(2)}) copy-start(bf16[227,512]{1,0:T(8,128)(2,1)} %param.21) | copy-start | bytes 697348
  229.4 31.4 %copy-start.26 = (bf16[512,512]{1,0:T(8,128)(2,1)S(1)}, bf16[512,512]{1,0:T(8,128)(2,1)}, u32[]{:S(2)}) copy-start(bf16[512,512]{1,0:T(8,128)(2,1)} %param.22) | copy-start | bytes 1572868
  257.2 3.6 copy-start.27
Sparse Core Ops, SparseCore 0:
  12.2 25.2 all-gather.1
  137.1 20.5 reduce-scatter.2
  225.2 31.9 reduce-scatter.4
  263.2 134.6 all-reduce.2
where the time goes:
time: 410 us; the launch traced here: 409 us
  waiting for transfers between devices  248 us (60%)
  other arithmetic  64.6 us (16%)
  local copies, waits for them, and re-layouts  30.7 us (7%)
  matrix products  23.6 us (6%)
  starting transfers between devices  21.9 us (5%)
  between operations  14.3 us (3%)
  blocking collectives  5.78 us (1%)
    psum x1, waiting for transfers between devices, body(): src_grad, edge_grad = lax.psum((src_part, edge_part), ('band', 'sub'))  135 us
    reduce_scatter x1, waiting for transfers between devices, return_grid(): lax.psum_scatter(middle.astype(jnp.bfloat16), 'sub', scatter_dimension=0,...  27.8 us
    ppermute x4, waiting for transfers between devices, from_behind(): lax.ppermute(value, axis, [(source, source + steps) for source in range(f...  25.8 us
    all_gather x1, waiting for transfers between devices, fetch_grid(): block = lax.all_gather(projected, 'sub', axis=0, tiled=True)  21.6 us
    scatter-add x1, other arithmetic, body(): jnp.zeros((grid_window.shape[0], latent), jnp.float32).at[grid_local]  21.5 us
    ppermute x2, waiting for transfers between devices, padded(): before = lax.ppermute(last, axis, up)  21.2 us
    reduce_scatter x1, waiting for transfers between devices, return_mesh(): lax.psum_scatter(middle.astype(jnp.bfloat16), 'sub', scatter_dimension=0,...  16.1 us
    ppermute x4, starting transfers between devices, from_behind(): lax.ppermute(value, axis, [(source, source + steps) for source in range(f...  11.2 us
  transfers between devices with their start and end apart: 12, of which 7 were waited for; matrix products, arithmetic and copies ran while one was open for 5% of the time, Pallas kernels for 0%

commit v1 on v0

--- a/solution.py
+++ b/solution.py
@@ -151,7 +151,7 @@
         jnp.bfloat16
     )
     grid_grad = times_transpose(w_embed, hidden_grad)
-    src_grad, edge_grad = lax.psum((src_part, edge_part), ("band", "sub"))
+    src_grad, edge_grad = lax.psum(lax.psum((src_part, edge_part), "sub"), "band")
     return (mesh_out, grid_grad, src_grad, edge_grad)
 
 

time: 410 us -> 430 us (1.049)
  waiting for transfers between devices: 248 us -> 268 us
    psum x1 -> x2, waiting for transfers between devices: 135 us -> 155 us  [the longest x1 104 us: body(): lax.psum(lax.psum((src_part, edge_part), 'sub'), 'band')]
  transfers between devices with their start and end apart: 12 -> 13, of which waited for: 7 -> 8; matrix products, arithmetic and copies ran while one was open for 5% -> 5% of each run, Pallas kernels for 0% -> 0%
where the time goes in v1:
time: 430 us; the launch traced here: 429 us
  waiting for transfers between devices  268 us (62%)
  other arithmetic  64.5 us (15%)
  local copies, waits for them, and re-layouts  30.7 us (7%)
  matrix products  23.6 us (5%)
  starting transfers between devices  22.2 us (5%)
  between operations  14.3 us (3%)
  blocking collectives  5.78 us (1%)
    psum x1, waiting for transfers between devices, body(): lax.psum(lax.psum((src_part, edge_part), 'sub'), 'band')  104 us
    psum x1, waiting for transfers between devices, body(): lax.psum((src_part, edge_part), 'sub')  51.5 us
    reduce_scatter x1, waiting for transfers between devices, return_grid(): lax.psum_scatter(middle.astype(jnp.bfloat16), 'sub', scatter_dimension=0,...  27.6 us
    ppermute x4, waiting for transfers between devices, from_behind(): lax.ppermute(value, axis, [(source, source + steps) for source in range(f...  25.8 us
    all_gather x1, waiting for transfers between devices, fetch_grid(): block = lax.all_gather(projected, 'sub', axis=0, tiled=True)  21.7 us
    scatter-add x1, other arithmetic, body(): jnp.zeros((grid_window.shape[0], latent), jnp.float32).at[grid_local]  21.5 us
    ppermute x2, waiting for transfers between devices, padded(): before = lax.ppermute(last, axis, up)  21.2 us
    reduce_scatter x1, waiting for transfers between devices, return_mesh(): lax.psum_scatter(middle.astype(jnp.bfloat16), 'sub', scatter_dimension=0,...  16.1 us
  transfers between devices with their start and end apart: 13, of which 8 were waited for; matrix products, arithmetic and copies ran while one was open for 5% of the time, Pallas kernels for 0%

profile of v1, /device:TPU:0, one launch (start us, length us, event | category | flops | bytes accessed | tf_op | source)
XLA Modules:
  0.0 428.6 jit_solution(8172003018930848113)
XLA Ops:
  7.3 1.4 fusion.53
  8.7 1.0 copy-done.8
  9.7 2.4 convolution_convert_fusion
  12.4 0.6 compare_and_fusion.1
  13.4 0.6 copy-done.6
  14.2 1.0 mul.82
  15.3 0.5 compare_and_fusion.2
  15.8 21.7 %all-gather.2.cloned.1.call-done = bf16[2048,512]{1,0:T(8,128)(2,1)} async-done(((bf16[512,512]{1,0:T(8,128)(2,1)}), bf16[2048,512]{1,0:T(8,128)(2,1)}) %all-gather.2.cloned.1.call-update) | async-done | bytes 2097168 | tf_op jit(solution)/shard_map/all_gather | solution.py:54
  37.5 1.3 fusion.48
  38.8 3.4 collective-permute-start
  42.2 1.3 collective-permute-start.1
  43.8 21.2 %collective-permute-done = bf16[512,512]{1,0:T(8,128)(2,1)S(1)} collective-permute-done((bf16[512,512]{1,0:T(8,128)(2,1)S(1)}, bf16[512,512]{1,0:T(8,128)(2,1)S(1)}, u32[]{:S(2)}, u32[]{:S(2)}) %collective-permute-start) | collective-permute-done | bytes 524320 | tf_op jit(solution)/shard_map/ppermute | solution.py:17
  65.0 3.0 pad_maximum_fusion
  67.9 10.6 %gather_fusion = bf16[2560,512]{1,0:T(8,128)(2,1)} fusion(bf16[3072,512]{1,0:T(8,128)(2,1)} %pad_maximum_fusion, s32[3072]{0:T(1024)S(1)} %pad_clamp_fusion), kind=kCustom, calls=%fused_computation | custom fusion | bytes 5253120 | tf_op jit(solution)/shard_map/jit(_take)/gather | solution.py:104
  78.6 5.7 %bitcast_add_fusion = (f32[2560,512]{1,0:T(8,128)}, bf16[2560,512]{1,0:T(8,128)(2,1)S(1)}) fusion(f32[64,512]{1,0:T(8,128)S(1)} %fusion.54, bf16[2560,512]{1,0:T(8,128)(2,1)} %gather_fusion, pred[2560]{0:T(1024)(128)(4,1)S(1)} %compare_and_fusion), kind=kLoop, calls=%fused_computation.10 | loop fusion | flops 10485760 | bytes 10619392 | tf_op jit(solution)/shard_map/add | solution.py:105
  84.2 1.6 fusion.51
  85.8 0.9 multiply_reduce_fusion
  86.8 3.5 subtract_divide_fusion
  90.3 3.4 reduce_sum.67
  93.7 1.3 convolution_convert_fusion.1
  95.0 5.8 %all_gather.7 = bf16[256,512]{1,0:T(8,128)(2,1)S(1)} all-gather(bf16[64,512]{1,0:T(8,128)(2,1)S(1)} %convolution_convert_fusion.1), channel_id=1, replica_groups=mesh['band'=8,'sub'=4] {'sub'}, dimensions={0}, use_global_device_ids=true | all-gather | bytes 327680 | tf_op jit(solution)/shard_map/all_gather | solution.py:117
  100.8 0.7 copy-done.5
  101.5 4.4 %collective-permute-start.2 = (bf16[64,512]{1,0:T(8,128)(2,1)S(1)}, bf16[64,512]{1,0:T(8,128)(2,1)S(1)}, u32[]{:S(2)}, u32[]{:S(2)}) collective-permute-start(bf16[64,512]{1,0:T(8,128)(2,1)S(1)} %get-tuple-element.68), channel_id=1, source_target_pairs={{0,4},{4,8},{8,12},{12,16},{16,20},{20,24},{24,28},{1,5},{5,9},{9,... | collective-permute-start | bytes 196616 | tf_op jit(solution)/shard_map/ppermute | solution.py:17
  105.9 1.5 collective-permute-start.3
  107.4 1.2 fusion.55
  108.6 0.6 copy-done.7
  109.3 1.1 add.190
  110.4 2.2 add.196
  112.6 0.6 copy-done.20
  113.2 1.0 pad_maximum_fusion.1
  114.3 2.6 gather_fusion.1
  116.8 5.1 %scatter_custom_fusion = f32[384,512]{1,0:T(8,128)} fusion(s32[384]{0:T(512)} %copy-done.23, f32[384,512]{1,0:T(8,128)} %mul.82, f32[384,512]{1,0:T(8,128)} %add.196, bf16[384,512]{1,0:T(8,128)(2,1)} %gather_fusion.1, f32[]{:T(128)} %constant.173.clone.1, f32[]{:T(128)} %constant.175.clone.1, pred[384]{0:T(512)(128)(4,1)} %compare_and_fusion.2, ...), kind=kCustom, calls=%fused_computation.47 | custom fusion | flops 2359296 | bytes 2754560 | tf_op jit(solution)/shard_map/scatter-add | solution.py:131
  121.9 1.2 convert.8
  123.1 4.9 %collective-permute-start.4 = (bf16[64,512]{1,0:T(8,128)(2,1)S(1)}, bf16[64,512]{1,0:T(8,128)(2,1)S(1)}, u32[]{:S(2)}, u32[]{:S(2)}) collective-permute-start(bf16[64,512]{1,0:T(8,128)(2,1)S(1)} %get-tuple-element.67), channel_id=1, source_target_pairs={{0,4},{4,8},{8,12},{12,16},{16,20},{20,24},{24,28},{1,5},{5,9},{9,... | collective-permute-start | bytes 196616 | tf_op jit(solution)/shard_map/ppermute | solution.py:26
  128.0 1.1 slice.134
  129.1 1.3 collective-permute-start.5
  130.4 0.9 fusion.41
  131.4 4.8 %collective-permute-done.5 = bf16[64,512]{1,0:T(8,128)(2,1)S(1)} collective-permute-done((bf16[64,512]{1,0:T(8,128)(2,1)S(1)}, bf16[64,512]{1,0:T(8,128)(2,1)S(1)}, u32[]{:S(2)}, u32[]{:S(2)}) %collective-permute-start.5) | collective-permute-done | bytes 65568 | tf_op jit(solution)/shard_map/ppermute | solution.py:26
  136.2 0.7 convert_element_type.88
  137.0 0.7 copy.18
  137.7 0.9 gather.12
  138.7 2.9 multiply_reduce_fusion.1
  141.6 16.1 %reduce-scatter.3.cloned.1.call-done = bf16[64,512]{1,0:T(8,128)(2,1)} async-done(((bf16[256,512]{1,0:T(8,128)(2,1)}), bf16[64,512]{1,0:T(8,128)(2,1)}) %reduce-scatter.3.cloned.1.call-update) | async-done | bytes 65552 | tf_op jit(solution)/shard_map/reduce_scatter | solution.py:83
  157.7 1.3 convolution_add_fusion.1
  159.0 1.4 fusion.52
  160.5 3.6 fusion.3
  164.3 3.9 fusion.2
  168.2 3.9 fusion.56
  172.1 21.5 %scatter_custom_fusion.1 = f32[3072,512]{1,0:T(8,128)} fusion(s32[2560]{0:T(1024)} %copy-done.21, f32[2560,512]{1,0:T(8,128)} %fusion.56, f32[2560,512]{1,0:T(8,128)} %get-tuple-element.62, f32[]{:T(128)} %constant.175.clone.1, f32[]{:T(128)} %constant.173.clone.1), kind=kCustom, calls=%fused_computation.11 | custom fusion | flops 11796480 | bytes 16778240 | tf_op jit(solution)/shard_map/scatter-add | solution.py:145
  193.7 3.2 convert.9
  197.0 3.7 collective-permute-start.6
  200.7 1.3 collective-permute-start.7
  202.0 21.0 %collective-permute-done.6 = bf16[512,512]{1,0:T(8,128)(2,1)S(1)} collective-permute-done((bf16[512,512]{1,0:T(8,128)(2,1)S(1)}, bf16[512,512]{1,0:T(8,128)(2,1)S(1)}, u32[]{:S(2)}, u32[]{:S(2)}) %collective-permute-start.6) | collective-permute-done | bytes 524320 | tf_op jit(solution)/shard_map/ppermute | solution.py:26
  223.1 0.3 fusion.16
  223.4 1.6 convert_element_type.93
  225.3 4.3 fusion.57
  229.6 27.6 %reduce-scatter.5.cloned.1.call-done = bf16[512,512]{1,0:T(8,128)(2,1)} async-done(((bf16[2048,512]{1,0:T(8,128)(2,1)}), bf16[512,512]{1,0:T(8,128)(2,1)}) %reduce-scatter.5.cloned.1.call-update) | async-done | bytes 524304 | tf_op jit(solution)/shard_map/reduce_scatter | solution.py:68
  257.2 2.9 fusion.46
  260.1 51.5 %all-reduce.7.cloned.1.call-done = (f32[512,512]{1,0:T(8,128)}, f32[512,512]{1,0:T(8,128)}) async-done(((f32[512,512]{1,0:T(8,128)}, f32[512,512]{1,0:T(8,128)}), (f32[512,512]{1,0:T(8,128)}, f32[512,512]{1,0:T(8,128)})) %all-reduce.7.cloned.1.call-update) | async-done | bytes 2097168 | tf_op jit(solution)/shard_map/psum | solution.py:154
  311.7 0.6 add_convert_fusion
  312.4 1.7 fusion.14
  314.0 103.6 %all-reduce.5.cloned.1.call-done = (f32[512,512]{1,0:T(8,128)}, f32[512,512]{1,0:T(8,128)}) async-done(((f32[512,512]{1,0:T(8,128)}, f32[512,512]{1,0:T(8,128)}), (f32[512,512]{1,0:T(8,128)}, f32[512,512]{1,0:T(8,128)})) %all-reduce.5.cloned.1.call-update) | async-done | bytes 2097168 | tf_op jit(solution)/shard_map/psum | solution.py:154
  417.6 2.3 copy.29
  419.8 2.3 copy.30
  (95 shorter events, 2.2 us)
Async XLA Ops:
  7.2 77.0 %copy-start = (bf16[512,512]{1,0:T(8,128)(2,1)S(1)}, bf16[512,512]{1,0:T(8,128)(2,1)}, u32[]{:S(2)}) copy-start(bf16[512,512]{1,0:T(8,128)(2,1)} %param.24) | copy-start | bytes 1572868
  7.2 4.9 %copy-start.22 = (s32[64,40]{0,1:T(8,128)S(1)}, s32[64,40]{0,1:T(8,128)}, u32[]{:S(2)}) copy-start(s32[64,40]{0,1:T(8,128)} %param.27) | copy-start | bytes 30724
  7.2 5.2 %copy-start.25 = (s32[64,6]{0,1:T(8,128)S(1)}, s32[64,6]{0,1:T(8,128)}, u32[]{:S(2)}) copy-start(s32[64,6]{0,1:T(8,128)} %param.28) | copy-start | bytes 4612
  7.2 6.2 %copy-start.14 = (bf16[64,512]{1,0:T(8,128)(2,1)S(1)}, bf16[64,512]{1,0:T(8,128)(2,1)}, u32[]{:S(2)}) copy-start(bf16[64,512]{1,0:T(8,128)(2,1)} %param.29) | copy-start | bytes 196612
  7.2 30.3 %all-gather.2.cloned.1.call-start = ((), (), s32[]{:S(2)}) async-start(), calls=%async_computation.2 | async-start | bytes 2621440 | tf_op jit(solution)/shard_map/all_gather | solution.py:54
  8.7 1.0 copy-start.8
  9.7 33.9 %copy-start.13 = (bf16[512,512]{1,0:T(8,128)(2,1)S(1)}, bf16[512,512]{1,0:T(8,128)(2,1)}, u32[]{:S(2)}) copy-start(bf16[512,512]{1,0:T(8,128)(2,1)} %param.23) | copy-start | bytes 1572868
  9.7 33.9 %copy-start.15 = (bf16[64,512]{1,0:T(8,128)(2,1)S(1)}, bf16[64,512]{1,0:T(8,128)(2,1)}, u32[]{:S(2)}) copy-start(bf16[64,512]{1,0:T(8,128)(2,1)} %param.20) | copy-start | bytes 196612
  12.1 145.6 %reduce-scatter.3.cloned.1.call-start = ((), (), s32[]{:S(2)}) async-start(), calls=%async_computation.3 | async-start | bytes 327680 | tf_op jit(solution)/shard_map/reduce_scatter | solution.py:83
  13.4 0.7 copy-start.6
  15.2 52.7 %copy-start.21 = (s32[2560]{0:T(1024)}, s32[2560]{0:T(1024)S(1)}, u32[]{:S(2)}) copy-start(s32[2560]{0:T(1024)S(1)} %fusion.43) | copy-start | bytes 30724
  15.3 28.2 %copy-start.23 = (s32[384]{0:T(512)}, s32[384]{0:T(512)S(1)}, u32[]{:S(2)}) copy-start(s32[384]{0:T(512)S(1)} %fusion.44) | copy-start | bytes 4612
  38.8 26.2 %collective-permute-start = (bf16[512,512]{1,0:T(8,128)(2,1)S(1)}, bf16[512,512]{1,0:T(8,128)(2,1)S(1)}, u32[]{:S(2)}, u32[]{:S(2)}) collective-permute-start(bf16[512,512]{1,0:T(8,128)(2,1)S(1)} %get-tuple-element.64), channel_id=1, source_target_pairs={{0,4},{4,8},{8,12},{12,16},{16,20},{20,24},{24,28},{1,5},{5,9},{9,... | collective-permute-start | bytes 1572872 | tf_op jit(solution)/shard_map/ppermute | solution.py:17
  42.2 22.8 %collective-permute-start.1 = (bf16[512,512]{1,0:T(8,128)(2,1)S(1)}, bf16[512,512]{1,0:T(8,128)(2,1)S(1)}, u32[]{:S(2)}, u32[]{:S(2)}) collective-permute-start(bf16[512,512]{1,0:T(8,128)(2,1)S(1)} %get-tuple-element.65), channel_id=1, source_target_pairs={{4,0},{8,4},{12,8},{16,12},{20,16},{24,20},{28,24},{5,1},{9,5},{13... | collective-permute-start | bytes 1572872 | tf_op jit(solution)/shard_map/ppermute | solution.py:18
  85.8 4.5 %copy-start.1 = (f32[2560,512]{1,0:T(8,128)}, f32[2560,512]{1,0:T(8,128)S(1)}, u32[]{:S(2)}) copy-start(f32[2560,512]{1,0:T(8,128)S(1)} %get-tuple-element.71) | copy-start | bytes 15728644
  86.8 3.5 copy-start.18
  90.3 3.4 copy-start.16
  93.7 13.7 %copy-start.10 = (bf16[64,512]{1,0:T(8,128)(2,1)}, bf16[64,512]{1,0:T(8,128)(2,1)S(1)}, u32[]{:S(2)}) copy-start(bf16[64,512]{1,0:T(8,128)(2,1)S(1)} %add_convert_fusion.1) | copy-start | bytes 196612
  100.8 0.7 copy-start.5
  101.5 11.1 %collective-permute-start.2 = (bf16[64,512]{1,0:T(8,128)(2,1)S(1)}, bf16[64,512]{1,0:T(8,128)(2,1)S(1)}, u32[]{:S(2)}, u32[]{:S(2)}) collective-permute-start(bf16[64,512]{1,0:T(8,128)(2,1)S(1)} %get-tuple-element.68), channel_id=1, source_target_pairs={{0,4},{4,8},{8,12},{12,16},{16,20},{20,24},{24,28},{1,5},{5,9},{9,... | collective-permute-start | bytes 196616 | tf_op jit(solution)/shard_map/ppermute | solution.py:17
  105.9 7.3 %collective-permute-start.3 = (bf16[64,512]{1,0:T(8,128)(2,1)S(1)}, bf16[64,512]{1,0:T(8,128)(2,1)}, u32[]{:S(2)}, u32[]{:S(2)}) collective-permute-start(bf16[64,512]{1,0:T(8,128)(2,1)S(1)} %get-tuple-element.69), channel_id=1, source_target_pairs={{4,0},{8,4},{12,8},{16,12},{20,16},{24,20},{28,24},{5,1},{9,5},{13... | collective-permute-start | bytes 196616 | tf_op jit(solution)/shard_map/ppermute | solution.py:18
  108.6 0.6 copy-start.7
  112.6 0.6 copy-start.20
  116.8 20.2 %copy-start.24 = (pred[64,6]{0,1:T(8,128)(4,1)S(1)}, pred[64,6]{0,1:T(8,128)(4,1)}, u32[]{:S(2)}) copy-start(pred[64,6]{0,1:T(8,128)(4,1)} %get-tuple-element.58) | copy-start | bytes 1156
  116.8 20.9 %copy-start.4 = (bf16[384,512]{1,0:T(8,128)(2,1)S(1)}, bf16[384,512]{1,0:T(8,128)(2,1)}, u32[]{:S(2)}) copy-start(bf16[384,512]{1,0:T(8,128)(2,1)} %gather_fusion.1) | copy-start | bytes 1179652
  123.1 7.3 %collective-permute-start.4 = (bf16[64,512]{1,0:T(8,128)(2,1)S(1)}, bf16[64,512]{1,0:T(8,128)(2,1)S(1)}, u32[]{:S(2)}, u32[]{:S(2)}) collective-permute-start(bf16[64,512]{1,0:T(8,128)(2,1)S(1)} %get-tuple-element.67), channel_id=1, source_target_pairs={{0,4},{4,8},{8,12},{12,16},{16,20},{20,24},{24,28},{1,5},{5,9},{9,... | collective-permute-start | bytes 196616 | tf_op jit(solution)/shard_map/ppermute | solution.py:26
  129.1 7.1 %collective-permute-start.5 = (bf16[64,512]{1,0:T(8,128)(2,1)S(1)}, bf16[64,512]{1,0:T(8,128)(2,1)S(1)}, u32[]{:S(2)}, u32[]{:S(2)}) collective-permute-start(bf16[64,512]{1,0:T(8,128)(2,1)S(1)} %get-tuple-element.66), channel_id=1, source_target_pairs={{4,0},{8,4},{12,8},{16,12},{20,16},{24,20},{28,24},{5,1},{9,5},{13... | collective-permute-start | bytes 196616 | tf_op jit(solution)/shard_map/ppermute | solution.py:26
  137.0 120.2 %reduce-scatter.5.cloned.1.call-start = ((), (), s32[]{:S(2)}) async-start(), calls=%async_computation.4 | async-start | bytes 2621440 | tf_op jit(solution)/shard_map/reduce_scatter | solution.py:68
  138.7 25.6 %copy-start.19 = (f32[2560]{0:T(1024)S(1)}, f32[2560]{0:T(1024)}, u32[]{:S(2)}) copy-start(f32[2560]{0:T(1024)} %copy-done.18) | copy-start | bytes 30724
  168.2 3.9 copy-start.3
  196.9 26.0 %copy-start.2 = (f32[3072,512]{1,0:T(8,128)S(1)}, f32[3072,512]{1,0:T(8,128)}, u32[]{:S(2)}) copy-start(f32[3072,512]{1,0:T(8,128)} %scatter_custom_fusion.1) | copy-start | bytes 18874372
  196.9 26.0 %slice-start = ((f32[3072,512]{1,0:T(8,128)}), f32[2048,512]{1,0:T(8,128)S(1)}, s32[]{:S(2)}) async-start(f32[3072,512]{1,0:T(8,128)} %scatter_custom_fusion.1), calls=%async_computation.7 | async-start | bytes 8388608 | tf_op jit(solution)/shard_map/slice | solution.py:59
  197.0 25.9 %collective-permute-start.6 = (bf16[512,512]{1,0:T(8,128)(2,1)S(1)}, bf16[512,512]{1,0:T(8,128)(2,1)S(1)}, u32[]{:S(2)}, u32[]{:S(2)}) collective-permute-start(bf16[512,512]{1,0:T(8,128)(2,1)S(1)} %get-tuple-element.61), channel_id=1, source_target_pairs={{0,4},{4,8},{8,12},{12,16},{16,20},{20,24},{24,28},{1,5},{5,9},{9,... | collective-permute-start | bytes 1572872 | tf_op jit(solution)/shard_map/ppermute | solution.py:26
  200.7 22.4 %collective-permute-start.7 = (bf16[512,512]{1,0:T(8,128)(2,1)S(1)}, bf16[512,512]{1,0:T(8,128)(2,1)S(1)}, u32[]{:S(2)}, u32[]{:S(2)}) collective-permute-start(bf16[512,512]{1,0:T(8,128)(2,1)S(1)} %get-tuple-element.60), channel_id=1, source_target_pairs={{4,0},{8,4},{12,8},{16,12},{20,16},{24,20},{28,24},{5,1},{9,5},{13... | collective-permute-start | bytes 1572872 | tf_op jit(solution)/shard_map/ppermute | solution.py:26
  225.0 86.6 %all-reduce.7.cloned.1.call-start = ((), (), s32[]{:S(2)}) async-start(), calls=%async_computation.6 | async-start | bytes 4194304 | tf_op jit(solution)/shard_map/psum | solution.py:154
  229.5 82.1 %copy-start.11 = (bf16[64,512]{1,0:T(8,128)(2,1)S(1)}, bf16[64,512]{1,0:T(8,128)(2,1)}, u32[]{:S(2)}) copy-start(bf16[64,512]{1,0:T(8,128)(2,1)} %copy-done.10) | copy-start | bytes 196612
  229.5 82.1 %copy-start.12 = (f32[64,512]{1,0:T(8,128)S(1)}, f32[64,512]{1,0:T(8,128)}, u32[]{:S(2)}) copy-start(f32[64,512]{1,0:T(8,128)} %get-tuple-element.53) | copy-start | bytes 393220
  229.5 82.8 %copy-start.9 = (f32[512,512]{1,0:T(8,128)S(1)}, f32[512,512]{1,0:T(8,128)}, u32[]{:S(2)}) copy-start(f32[512,512]{1,0:T(8,128)} %copy-done.8) | copy-start | bytes 3145732
  229.5 82.8 %copy-start.17 = (bf16[227,512]{1,0:T(8,128)(2,1)S(1)}, bf16[227,512]{1,0:T(8,128)(2,1)}, u32[]{:S(2)}) copy-start(bf16[227,512]{1,0:T(8,128)(2,1)} %param.21) | copy-start | bytes 697348
  229.5 82.8 %copy-start.26 = (bf16[512,512]{1,0:T(8,128)(2,1)S(1)}, bf16[512,512]{1,0:T(8,128)(2,1)}, u32[]{:S(2)}) copy-start(bf16[512,512]{1,0:T(8,128)(2,1)} %param.22) | copy-start | bytes 1572868
  257.2 55.2 %copy-start.27 = (bf16[512,512]{1,0:T(8,128)(2,1)S(1)}, bf16[512,512]{1,0:T(8,128)(2,1)}, u32[]{:S(2)}) copy-start(bf16[512,512]{1,0:T(8,128)(2,1)} %reduce-scatter.5.cloned.1.call-done) | copy-start | bytes 1572868
  260.1 157.5 %all-reduce.5.cloned.1.call-start = ((), (), s32[]{:S(2)}) async-start(), calls=%async_computation.5 | async-start | bytes 4194304 | tf_op jit(solution)/shard_map/psum | solution.py:154
Sparse Core Ops, SparseCore 0:
  12.2 25.2 all-gather.1
  137.1 20.5 reduce-scatter.2
  225.1 31.9 reduce-scatter.4
  260.2 51.4 all-reduce.6
  315.2 102.3 all-reduce.4
